TPU v7x, 256 devices: a whole 4x4x8 slice. The times are simulated.
256 devices in a mesh: dp: 4 (over y_hi, core), seq: 64 (over z, x, y_lo).
Axes of the slice: x: 4, y: 4 (y_hi: 2, y_lo: 2; y = y_hi * 2 + y_lo), z: 8, core: 2. Of those that a mesh axis runs over, the one named last changes fastest.
Arguments:
- queries: bfloat16 [4, 8192, 2048], P('dp', 'seq'), may hold values from -12 to 12
- keys: bfloat16 [4, 8192, 512], P('dp', 'seq'), may hold values from -4 to 4
- values: bfloat16 [4, 8192, 512], P('dp', 'seq'), may hold values from -6 to 6
- segments: int32 [4, 8192], P('dp', 'seq'), may hold values from 0 to 3, never falling along the last dimension, each value on 1 to 7168 neighbouring positions
- task_ids: int32 [4], replicated, may hold values from 0 to 127
- prompt_keys: bfloat16 [128, 128, 512], P('seq'), may hold values from -4 to 4
- prompt_values: bfloat16 [128, 128, 512], P('seq'), may hold values from -6 to 6
- grad_out: bfloat16 [4, 8192, 2048], P('dp', 'seq'), may hold values from -6 to 6
Outputs:
- attended: bfloat16 [4, 8192, 2048], P('dp', 'seq')
- prompt_key_grad: float32 [128, 128, 512], P('seq')
- prompt_value_grad: float32 [128, 128, 512], P('seq')
Inputs may be any that keep to these rules, and one draw needn't show every extreme that they name: `segments`: along each example the document numbers never fall; one document holds 7168 tokens.
All inputs are finite; a program needn't handle non-finite values.
Results may differ from a plain program's by a relative error of at most 0.0096.
Values may be sent and summed in bfloat16 or wider, within the bound.
No kernel may reach another device: no remote copies, remote signals or barrier semaphores. Data moves between devices by JAX's collectives and lax.ppermute only.
A program may use at most 128 MiB of HBM per device.

v0:
```python
import math
import jax
import jax.numpy as jnp
from jax import lax
from jax.sharding import Mesh
from jax.sharding import PartitionSpec as P

KVH = 4
GROUP = 4
HD = 128
PROMPT = 128
SEQ = ("seq_0", "seq_1", "seq_2")
DP_SEQ = ("dp", "seq_0", "seq_1", "seq_2")


def laid_out(blocks, dim):
    blocks = jnp.moveaxis(blocks, 0, dim)
    lengths = blocks.shape
    return blocks.reshape(*lengths[:dim], lengths[dim] * lengths[dim + 1], *lengths[dim + 2 :])


def sent_to_all(shard, axis):
    devices = lax.axis_size(axis)
    return lax.all_to_all(
        jnp.broadcast_to(shard[None], (devices, *shard.shape)), axis, 0, 0, tiled=True
    )


def gather_directly(shard, axis, dim):
    return laid_out(sent_to_all(shard, axis), dim)


def broadcast_by_axis(shard, axes, root):
    shard = jnp.where(lax.axis_index(axes) == root, shard, jnp.zeros_like(shard))
    for axis in axes:
        shard = lax.psum(shard, axis)
    return shard


def piece_ends(length, count):
    unit = 8 if length >= 8 * count else 1
    return [length // unit * k // count * unit for k in range(1, count)]


def gather_in_order(shard, axes, turns):
    blocks = shard
    for k in turns:
        blocks = lax.all_gather(blocks, axes[k])
    done = turns[::-1]
    back = [done.index(k) for k in range(len(axes))]
    blocks = blocks.transpose(*back, *range(len(axes), blocks.ndim))
    return blocks.reshape(-1, *shard.shape)


def gather_all_axes(shard, axes, dim):
    cut = max(range(max(1, shard.ndim - 1)), key=lambda d: shard.shape[d])
    count, gathered = (len(axes), [])
    for initial, piece in enumerate(
        jnp.split(shard, piece_ends(shard.shape[cut], count), axis=cut)
    ):
        if piece.size:
            turns = [(initial - k) % count for k in range(count)]
            gathered.append(gather_in_order(piece, axes, turns))
    return laid_out(jnp.concatenate(gathered, axis=cut + 1), dim)


def shards(queries, keys, values, segments, task_ids, prompt_keys, prompt_values, grad_out):
    tok_rows = queries.shape[1]
    scaling = 1.0 / math.sqrt(HD)
    seq_rank = lax.axis_index(SEQ)
    query_heads = queries[0].reshape(tok_rows, KVH, GROUP, HD)
    query_segments = segments[0]
    query_index = seq_rank * tok_rows + lax.iota(jnp.int32, tok_rows)
    all_segments = gather_directly(segments[0], SEQ, 0)
    bank_size = prompt_keys.shape[0]
    my_task = task_ids[lax.axis_index("dp")]
    prompt_owner = my_task // bank_size
    bank_slot = my_task % bank_size
    local_pair = jnp.stack(
        [
            lax.dynamic_index_in_dim(prompt_keys, bank_slot, 0, keepdims=False),
            lax.dynamic_index_in_dim(prompt_values, bank_slot, 0, keepdims=False),
        ]
    )
    shared_pair = broadcast_by_axis(local_pair, SEQ, prompt_owner)
    prompt_key_heads = shared_pair[0].reshape(PROMPT, KVH, HD)
    prompt_value_heads = shared_pair[1].reshape(PROMPT, KVH, HD)
    prompt_scores = (
        jnp.einsum(
            "tkgd,pkd->tkgp", query_heads, prompt_key_heads, preferred_element_type=jnp.float32
        )
        * scaling
    )
    maximum = jnp.max(prompt_scores, axis=-1)
    weights = jnp.exp(prompt_scores - maximum[..., None])
    totals = jnp.sum(weights, axis=-1)
    accumulated = jnp.einsum(
        "tkgp,pkd->tkgd",
        weights.astype(jnp.bfloat16),
        prompt_value_heads,
        preferred_element_type=jnp.float32,
    )
    carried = (maximum, totals, accumulated)

    def absorb_rows(state_now, stacked, first_row):
        key_count = stacked.shape[1]
        key_index = first_row + lax.iota(jnp.int32, key_count)
        key_segments = lax.dynamic_slice_in_dim(
            all_segments, jnp.maximum(first_row, 0), key_count, 0
        )
        key_mask = (
            (key_segments[None, :] == query_segments[:, None])
            & (key_index[None, :] <= query_index[:, None])
            & True
        )

        def update(inner_state):
            old_peak, old_totals, old_accum = inner_state
            key_heads = stacked[0].reshape(key_count, KVH, HD)
            value_heads = stacked[1].reshape(key_count, KVH, HD)
            scores = (
                jnp.einsum(
                    "tkgd,skd->tkgs", query_heads, key_heads, preferred_element_type=jnp.float32
                )
                * scaling
            )
            mask_wide = key_mask[:, None, None, :]
            new_peak = jnp.maximum(
                old_peak, jnp.max(jnp.where(mask_wide, scores, -jnp.inf), axis=-1)
            )
            shrink = jnp.exp(old_peak - new_peak)
            block_weights = jnp.where(mask_wide, jnp.exp(scores - new_peak[..., None]), 0.0)
            new_totals = old_totals * shrink + jnp.sum(block_weights, axis=-1)
            new_accum = old_accum * shrink[..., None] + jnp.einsum(
                "tkgs,skd->tkgd",
                block_weights.astype(jnp.bfloat16),
                value_heads,
                preferred_element_type=jnp.float32,
            )
            return (new_peak, new_totals, new_accum)

        return lax.cond(jnp.any(key_mask), update, lambda inner_state: inner_state, state_now)

    own_pair = jnp.stack([keys[0], values[0]])
    stacked = gather_all_axes(own_pair, SEQ, 1)
    key_count = stacked.shape[1]
    tile_rows = 512

    def loop_tile(block_index, inner_state):
        offset = block_index * tile_rows
        piece = lax.dynamic_slice_in_dim(stacked, offset, tile_rows, 1)
        return absorb_rows(inner_state, piece, offset)

    carried = lax.fori_loop(0, key_count // tile_rows, loop_tile, carried)
    maximum, totals, accumulated = carried
    attended = (accumulated / totals[..., None]).astype(jnp.bfloat16)
    log_norm = maximum + jnp.log(totals)
    grad_heads = grad_out[0].reshape(tok_rows, KVH, GROUP, HD)
    attended_wide = lax.optimization_barrier(attended).astype(jnp.float32)
    row_delta = jnp.sum(grad_heads.astype(jnp.float32) * attended_wide, axis=-1)
    prompt_probs = jnp.exp(prompt_scores - log_norm[..., None])
    prompt_dots = jnp.einsum(
        "tkgd,pkd->tkgp", grad_heads, prompt_value_heads, preferred_element_type=jnp.float32
    )
    score_grad = prompt_probs * (prompt_dots - row_delta[..., None])
    value_part = jnp.einsum(
        "tkgp,tkgd->pkd",
        prompt_probs.astype(jnp.bfloat16),
        grad_heads,
        preferred_element_type=jnp.float32,
    )
    key_part = (
        jnp.einsum(
            "tkgp,tkgd->pkd",
            score_grad.astype(jnp.bfloat16),
            query_heads,
            preferred_element_type=jnp.float32,
        )
        * scaling
    )
    value_part = value_part.reshape(PROMPT, KVH * HD)
    key_part = key_part.reshape(PROMPT, KVH * HD)
    group_size = lax.axis_size("dp")
    group_rank = lax.axis_index("dp")
    slot_match = (lax.iota(jnp.int32, group_size) == group_rank)[:, None, None]
    key_buffer = jnp.where(slot_match, key_part[None], 0.0)
    value_buffer = jnp.where(slot_match, value_part[None], 0.0)
    key_all, value_all = lax.psum((key_buffer, value_buffer), DP_SEQ)
    own_tasks = seq_rank * bank_size + lax.iota(jnp.int32, bank_size)
    matches = (task_ids[:, None] == own_tasks[None, :])[:, :, None, None]
    key_grad = jnp.sum(jnp.where(matches, key_all[:, None], 0.0), axis=0)
    value_grad = jnp.sum(jnp.where(matches, value_all[:, None], 0.0), axis=0)
    return (attended.reshape(1, tok_rows, KVH * GROUP * HD), key_grad, value_grad)


def solution(mesh):
    split = Mesh(mesh.devices.reshape(mesh.shape["dp"], 8, 4, 2), ("dp", "seq_0", "seq_1", "seq_2"))
    return jax.shard_map(
        shards,
        mesh=split,
        in_specs=(
            P("dp", SEQ, None),
            P("dp", SEQ, None),
            P("dp", SEQ, None),
            P("dp", SEQ),
            P(),
            P(SEQ, None, None),
            P(SEQ, None, None),
            P("dp", SEQ, None),
        ),
        out_specs=(P("dp", SEQ, None), P(SEQ, None, None), P(SEQ, None, None)),
        check_vma=False,
    )
```

profile of v0, /device:TPU:2, one launch (start us, length us, event | category | flops | bytes accessed | tf_op | source)
XLA Modules:
  0.0 886.4 jit_solution(14403823708301323526)
XLA Ops:
  8.0 1.2 dynamic_slice.28
  11.9 1.0 constant_dynamic-slice_fusion.2
  13.2 0.7 maximum_select_fusion
  14.0 0.9 constant_dynamic-update-slice_fusion.1
  14.9 0.9 constant_dynamic-update-slice_fusion
  15.8 74.2 %all-reduce.6.cloned.1.call-done = bf16[2,128,512]{1,2,0:T(8,128)(2,1)} async-done(((bf16[2,128,512]{1,2,0:T(8,128)(2,1)}), bf16[2,128,512]{1,2,0:T(8,128)(2,1)}) %all-reduce.6.cloned.1.call-update) | async-done | bytes 262160 | tf_op jit(solution)/shard_map/psum | solution.py:36
  90.2 27.7 %all-gather = bf16[16,40,512]{2,1,0:T(8,128)(2,1)} all-gather(bf16[2,40,512]{2,1,0:T(8,128)(2,1)S(1)} %get-tuple-element.363), channel_id=2, replica_groups=mesh['dp'=4,'seq_0'=8,'seq_1'=4,'seq_2'=2] {'seq_0'}, dimensions={0}, use_global_device_ids=true | all-gather | bytes 737280 | tf_op jit(solution)/shard_map/all_gather | solution.py:48
  117.9 13.2 %all-gather.3 = bf16[8,40,512]{2,1,0:T(8,128)(2,1)} all-gather(bf16[2,40,512]{2,1,0:T(8,128)(2,1)S(1)} %get-tuple-element.364), channel_id=5, replica_groups=mesh['dp'=4,'seq_0'=8,'seq_1'=4,'seq_2'=2] {'seq_1'}, dimensions={0}, use_global_device_ids=true | all-gather | bytes 409600 | tf_op jit(solution)/shard_map/all_gather | solution.py:48
  131.2 5.5 all-reduce.8.cloned.1.call-done
  136.7 9.0 %all-gather.15.cloned.1.call-done = bf16[16,2,40,512]{3,2,1,0:T(8,128)(2,1)} async-done(((bf16[8,2,40,512]{3,2,1,0:T(8,128)(2,1)}), bf16[16,2,40,512]{3,2,1,0:T(8,128)(2,1)}) %all-gather.15.cloned.1.call-update) | async-done | bytes 1310736 | tf_op jit(solution)/shard_map/all_gather | solution.py:48
  145.8 44.8 %all-gather.19.cloned.1.call-done = bf16[32,2,40,512]{3,2,1,0:T(8,128)(2,1)} async-done(((bf16[4,2,40,512]{3,2,1,0:T(8,128)(2,1)}), bf16[32,2,40,512]{3,2,1,0:T(8,128)(2,1)}) %all-gather.19.cloned.1.call-update) | async-done | bytes 2621456 | tf_op jit(solution)/shard_map/all_gather | solution.py:48
  190.7 5.3 all-gather.6
  196.0 14.8 %all-gather.7 = bf16[8,2,48,512]{3,2,1,0:T(8,128)(2,1)} all-gather(bf16[2,2,48,512]{3,2,1,0:T(8,128)(2,1)S(1)} %bitcast.153), channel_id=9, replica_groups=mesh['dp'=4,'seq_0'=8,'seq_1'=4,'seq_2'=2] {'seq_1'}, dimensions={0}, use_global_device_ids=true | all-gather | bytes 983040 | tf_op jit(solution)/shard_map/all_gather | solution.py:48
  210.9 0.6 broadcast_in_dim.114
  211.5 8.6 all-to-all-start
  220.2 0.3 copy.144
  220.4 0.3 copy.152
  220.7 0.3 copy.154
  221.0 5.4 all-reduce.10.cloned.1.call-done
  226.4 1.0 fusion.40
  227.4 0.4 fusion.41
  227.7 1.3 convolution_bitcast_fusion.1
  229.0 2.6 copy.151
  231.6 0.2 fusion.29
  231.8 56.3 %all-gather.17.cloned.1.call-done = bf16[8,8,2,40,512]{4,3,2,1,0:T(8,128)(2,1)} async-done(((bf16[2,8,2,40,512]{4,3,2,1,0:T(8,128)(2,1)}), bf16[8,8,2,40,512]{4,3,2,1,0:T(8,128)(2,1)}) %all-gather.17.cloned.1.call-update) | async-done | bytes 5242896 | tf_op jit(solution)/shard_map/all_gather | solution.py:48
  288.1 5.3 copy.148
  293.4 71.0 %all-gather.21.cloned.1.call-done = bf16[16,4,2,40,512]{4,3,2,1,0:T(8,128)(2,1)} async-done(((bf16[8,4,2,40,512]{4,3,2,1,0:T(8,128)(2,1)}), bf16[16,4,2,40,512]{4,3,2,1,0:T(8,128)(2,1)}) %all-gather.21.cloned.1.call-update) | async-done | bytes 5242896 | tf_op jit(solution)/shard_map/all_gather | solution.py:48
  364.4 5.3 copy.149
  369.7 72.0 %all-gather.23.cloned.1.call-done = bf16[32,2,2,48,512]{4,3,2,1,0:T(8,128)(2,1)} async-done(((bf16[4,2,2,48,512]{4,3,2,1,0:T(8,128)(2,1)}), bf16[32,2,2,48,512]{4,3,2,1,0:T(8,128)(2,1)}) %all-gather.23.cloned.1.call-update) | async-done | bytes 6291472 | tf_op jit(solution)/shard_map/all_gather | solution.py:48
  441.6 13.6 %maximum_bitcast_fusion = bf16[2,64,128,512]{3,2,0,1:T(8,128)(2,1)} fusion(bf16[64,2,48,512]{3,2,1,0:T(8,128)(2,1)} %bitcast.137, bf16[64,2,40,512]{3,2,1,0:T(8,128)(2,1)} %bitcast.129, bf16[64,2,40,512]{3,2,1,0:T(8,128)(2,1)} %bitcast.128), kind=kLoop, calls=%fused_computation.24 | loop fusion | flops 50331648 | bytes 33554432 | tf_op jit(solution)/shard_map/transpose | solution.py:17
  455.3 23.1 %copy.150 = bf16[2,64,128,512]{2,1,3,0:T(8,128)(2,1)} copy(bf16[2,64,128,512]{3,2,0,1:T(8,128)(2,1)} %maximum_bitcast_fusion) | data formatting | bytes 33554432 | tf_op jit(solution)/shard_map/transpose | solution.py:17
  478.4 25.3 %reshape.89 = bf16[2,8192,512]{1,2,0:T(8,128)(2,1)} reshape(bf16[2,64,128,512]{2,1,3,0:T(8,128)(2,1)} %copy.150) | data formatting | bytes 33554432 | tf_op jit(solution)/shard_map/reshape | solution.py:19
  503.7 32.3 %while.18 = (s32[]{:T(128)}, f32[128,4,4]{0,2,1:T(4,128)S(1)}, f32[128,4,4]{0,2,1:T(4,128)S(1)}, f32[128,4,4,128]{3,0,2,1:T(8,128)}, s32[8192]{0:T(1024)S(1)}, /...) while((s32[]{:T(128)}, f32[128,4,4]{0,2,1:T(4,128)S(1)}, ...), condition=%wide.region_11.12_spmd.clone, body=%wide.region_5.11_spmd.clone.sunk | while | flops 549196416 | bytes 27144060 | solution.py:154
  503.8 0.9 fusion.53
  505.4 5.6 conditional.3
  505.4 1.3 constant_dynamic-slice_fusion.1
  506.7 0.9 fusion.2
  507.5 0.9 fusion.6
  508.4 1.5 fusion.16
  510.0 1.0 copy-done.1
  511.0 0.9 fusion.53
  512.7 0.9 fusion.53
  514.4 0.9 fusion.53
  516.0 0.9 fusion.53
  517.7 0.9 fusion.53
  519.4 0.9 fusion.53
  521.1 0.9 fusion.53
  522.7 0.9 fusion.53
  524.4 0.9 fusion.53
  526.1 0.9 fusion.53
  527.8 0.9 fusion.53
  529.4 0.9 fusion.53
  531.1 0.9 fusion.53
  532.8 0.9 fusion.53
  534.4 0.9 fusion.53
  536.0 2.5 copy.153
  538.5 1.3 divide_convert_fusion
  539.9 0.2 multiply_reduce_fusion
  540.1 0.3 fusion.31
  540.4 0.6 fusion.27
  541.2 1.7 broadcast_select_fusion.1
  543.0 1.0 copy.161
  544.0 332.2 %all-reduce.12.cloned.1.call-done = (f32[4,128,512]{2,1,0:T(8,128)}, f32[4,128,512]{2,1,0:T(8,128)}) async-done(((f32[4,128,512]{2,1,0:T(8,128)}, f32[4,128,512]{2,1,0:T(8,128)}), (f32[4,128,512]{2,1,0:T(8,128)}, f32[4,128,512]{2,1,0:T(8,128)})) %all-reduce.12.cloned.1.call-update) | async-done | bytes 2097168 | tf_op jit(solution)/shard_map/psum | solution.py:188
  876.3 3.0 select_reduce_fusion
  (106 shorter events, 2.9 us)
Async XLA Ops:
  8.0 82.1 %all-reduce.6.cloned.1.call-start = ((), (), s32[]{:S(2)}) async-start(), calls=%async_computation.1 | async-start | bytes 524288 | tf_op jit(solution)/shard_map/psum | solution.py:36
  13.9 122.7 %all-reduce.8.cloned.1.call-start = ((), (), s32[]{:S(2)}) async-start(), calls=%async_computation.2 | async-start | bytes 524288 | tf_op jit(solution)/shard_map/psum | solution.py:36
  90.1 55.7 %all-gather.15.cloned.1.call-start = ((), (), s32[]{:S(2)}) async-start(), calls=%async_computation.4 | async-start | bytes 1966080 | tf_op jit(solution)/shard_map/all_gather | solution.py:48
  90.1 120.7 %copy-start.4 = (s32[1,128]{1,0:T(1,128)S(1)}, s32[1,128]{1,0:T(1,128)}, u32[]{:S(2)}) copy-start(s32[1,128]{1,0:T(1,128)} %param.15) | copy-start | bytes 1540
  90.1 130.0 %copy-start.2 = (bf16[1,128,2048]{2,1,0:T(8,128)(2,1)S(1)}, bf16[1,128,2048]{2,1,0:T(8,128)(2,1)}, u32[]{:S(2)}) copy-start(bf16[1,128,2048]{2,1,0:T(8,128)(2,1)} %param.12) | copy-start | bytes 1572868
  117.8 72.8 %all-gather.19.cloned.1.call-start = ((), (), s32[]{:S(2)}) async-start(), calls=%async_computation.6 | async-start | bytes 2949120 | tf_op jit(solution)/shard_map/all_gather | solution.py:48
  131.1 95.2 %all-reduce.10.cloned.1.call-start = ((), (), s32[]{:S(2)}) async-start(), calls=%async_computation.3 | async-start | bytes 524288 | tf_op jit(solution)/shard_map/psum | solution.py:36
  136.7 151.4 %all-gather.17.cloned.1.call-start = ((), (), s32[]{:S(2)}) async-start(), calls=%async_computation.5 | async-start | bytes 6553600 | tf_op jit(solution)/shard_map/all_gather | solution.py:48
  145.8 75.0 %copy-start.3 = (bf16[1,128,2048]{2,1,0:T(8,128)(2,1)S(1)}, bf16[1,128,2048]{2,1,0:T(8,128)(2,1)}, u32[]{:S(2)}) copy-start(bf16[1,128,2048]{2,1,0:T(8,128)(2,1)} %param.19) | copy-start | bytes 1572868
  145.8 218.6 %all-gather.21.cloned.1.call-start = ((), (), s32[]{:S(2)}) async-start(), calls=%async_computation.7 | async-start | bytes 7864320 | tf_op jit(solution)/shard_map/all_gather | solution.py:48
  190.6 251.0 %all-gather.23.cloned.1.call-start = ((), (), s32[]{:S(2)}) async-start(), calls=%async_computation.8 | async-start | bytes 7077888 | tf_op jit(solution)/shard_map/all_gather | solution.py:48
  211.5 292.2 %all-to-all-start = ((s32[64,1,128]{2,1,0:T(1,128)}), s32[64,1,128]{2,1,0:T(1,128)S(1)}, u32[]{:S(2)}, u32[]{:S(2)}) async-start(s32[64,1,128]{2,1,0:T(1,128)} %broadcast_in_dim.114), calls=%async_computation | async-start | bytes 65536 | tf_op jit(solution)/shard_map/all_to_all | solution.py:24
  220.1 656.2 %all-reduce.12.cloned.1.call-start = ((), (), s32[]{:S(2)}) async-start(), calls=%async_computation.9 | async-start | bytes 4194304 | tf_op jit(solution)/shard_map/psum | solution.py:188
  506.7 1.8 copy-start
  510.0 1.0 copy-start.1
  540.4 2.5 copy-start.5
Sparse Core Ops, SparseCore 0:
  14.1 75.9 all-reduce.5
  92.4 44.2 all-reduce.7
  543.1 333.1 all-reduce.11
Sparse Core Ops, SparseCore 1:
  117.9 27.8 all-gather.14
  147.4 43.1 all-gather.18
  193.1 33.3 all-reduce.9
  228.2 59.8 all-gather.16
  289.9 74.5 all-gather.20
  366.2 75.4 all-gather.22
where the time goes:
time: 889 us; the launch traced here: 886 us
  waiting for transfers between devices  670 us (75%)
  local copies, waits for them, and re-layouts  75.8 us (9%)
  blocking collectives  61 us (7%)
  other arithmetic  36.2 us (4%)
  between operations  18.1 us (2%)
  loops' own time  10.9 us (1%)
  starting transfers between devices  8.97 us (1%)
    psum x1, waiting for transfers between devices, shards(): key_all, value_all = lax.psum((key_buffer, value_buffer), DP_SEQ)  332 us
    all_gather x5, waiting for transfers between devices, gather_in_order(): blocks = lax.all_gather(blocks, axes[k])  253 us
    psum x3, waiting for transfers between devices, broadcast_by_axis(): shard = lax.psum(shard, axis)  85 us
    all_gather x4, blocking collectives, gather_in_order(): blocks = lax.all_gather(blocks, axes[k])  61 us
    reshape x1, local copies, waits for them, and re-layouts, laid_out(): blocks.reshape(*lengths[:dim], lengths[dim] * lengths[dim + 1], *lengths[...  25.3 us
    transpose x1, local copies, waits for them, and re-layouts, laid_out(): blocks = jnp.moveaxis(blocks, 0, dim)  23.1 us
  transfers between devices with their start and end apart: 10, of which 9 were waited for; matrix products, arithmetic and copies ran while one was open for 9% of the time, Pallas kernels for 0%

commit v1 on v0

--- a/solution.py
+++ b/solution.py
@@ -33,7 +33,7 @@
 def broadcast_by_axis(shard, axes, root):
     shard = jnp.where(lax.axis_index(axes) == root, shard, jnp.zeros_like(shard))
     for axis in axes:
-        shard = lax.psum(shard, axis)
+        shard = jnp.sum(lax.all_gather(shard, axis), axis=0)
     return shard
 
 

time: 889 us -> 822 us (0.925)
  waiting for transfers between devices: 670 us -> 589 us
  blocking collectives: 61 us -> 74 us
    psum x3 -> x0, waiting for transfers between devices: 85 us -> none  [broadcast_by_axis(): shard = lax.psum(shard, axis)]
  transfers between devices with their start and end apart: 10 -> 9, of which waited for: 9 -> 6; matrix products, arithmetic and copies ran while one was open for 9% -> 11% of each run, Pallas kernels for 0% -> 0%
where the time goes in v1:
time: 822 us; the launch traced here: 819 us
  waiting for transfers between devices  589 us (72%)
  local copies, waits for them, and re-layouts  75 us (9%)
  blocking collectives  74 us (9%)
  other arithmetic  39.5 us (5%)
  between operations  17 us (2%)
  loops' own time  11.3 us (1%)
  starting transfers between devices  8.83 us (1%)
    psum x1, waiting for transfers between devices, shards(): key_all, value_all = lax.psum((key_buffer, value_buffer), DP_SEQ)  333 us
    all_gather x5, waiting for transfers between devices, gather_in_order(): blocks = lax.all_gather(blocks, axes[k])  256 us
    all_gather x4, blocking collectives, gather_in_order(): blocks = lax.all_gather(blocks, axes[k])  66.7 us
    reshape x1, local copies, waits for them, and re-layouts, laid_out(): blocks.reshape(*lengths[:dim], lengths[dim] * lengths[dim + 1], *lengths[...  25.3 us
    transpose x1, local copies, waits for them, and re-layouts, laid_out(): blocks = jnp.moveaxis(blocks, 0, dim)  23.2 us
  transfers between devices with their start and end apart: 9, of which 6 were waited for; matrix products, arithmetic and copies ran while one was open for 11% of the time, Pallas kernels for 0%

profile of v1, /device:TPU:2, one launch (start us, length us, event | category | flops | bytes accessed | tf_op | source)
XLA Modules:
  0.0 819.4 jit_solution(6419911136234508713)
XLA Ops:
  7.2 1.2 dynamic_slice.28
  11.1 1.0 dynamic-slice_bitcast_fusion
  12.1 0.7 maximum_select_fusion
  12.9 0.9 constant_dynamic-update-slice_fusion.1
  13.8 0.9 constant_dynamic-update-slice_fusion
  14.8 32.7 %all-gather.2 = bf16[16,40,512]{2,1,0:T(8,128)(2,1)} all-gather(bf16[2,40,512]{2,1,0:T(8,128)(2,1)S(1)} %get-tuple-element.363), channel_id=4, replica_groups=mesh['dp'=4,'seq_0'=8,'seq_1'=4,'seq_2'=2] {'seq_0'}, dimensions={0}, use_global_device_ids=true | all-gather | bytes 737280 | tf_op jit(solution)/shard_map/all_gather | solution.py:48
  47.5 13.0 %all-gather.5 = bf16[8,40,512]{2,1,0:T(8,128)(2,1)} all-gather(bf16[2,40,512]{2,1,0:T(8,128)(2,1)S(1)} %get-tuple-element.364), channel_id=7, replica_groups=mesh['dp'=4,'seq_0'=8,'seq_1'=4,'seq_2'=2] {'seq_1'}, dimensions={0}, use_global_device_ids=true | all-gather | bytes 409600 | tf_op jit(solution)/shard_map/all_gather | solution.py:48
  60.7 2.7 reduce_sum.82
  63.4 24.4 %all-gather.23.cloned.1.call-done = bf16[16,2,40,512]{3,2,1,0:T(8,128)(2,1)} async-done(((bf16[8,2,40,512]{3,2,1,0:T(8,128)(2,1)}), bf16[16,2,40,512]{3,2,1,0:T(8,128)(2,1)}) %all-gather.23.cloned.1.call-update) | async-done | bytes 1310736 | tf_op jit(solution)/shard_map/all_gather | solution.py:48
  87.9 44.9 %all-gather.27.cloned.1.call-done = bf16[32,2,40,512]{3,2,1,0:T(8,128)(2,1)} async-done(((bf16[4,2,40,512]{3,2,1,0:T(8,128)(2,1)}), bf16[32,2,40,512]{3,2,1,0:T(8,128)(2,1)}) %all-gather.27.cloned.1.call-update) | async-done | bytes 2621456 | tf_op jit(solution)/shard_map/all_gather | solution.py:48
  132.8 5.3 all-gather.8
  138.1 15.7 %all-gather.9 = bf16[8,2,48,512]{3,2,1,0:T(8,128)(2,1)} all-gather(bf16[2,2,48,512]{3,2,1,0:T(8,128)(2,1)S(1)} %bitcast.161), channel_id=11, replica_groups=mesh['dp'=4,'seq_0'=8,'seq_1'=4,'seq_2'=2] {'seq_1'}, dimensions={0}, use_global_device_ids=true | all-gather | bytes 983040 | tf_op jit(solution)/shard_map/all_gather | solution.py:48
  153.9 0.6 broadcast_in_dim.114
  154.5 8.5 %all-to-all-start = ((s32[64,1,128]{2,1,0:T(1,128)}), s32[64,1,128]{2,1,0:T(1,128)S(1)}, u32[]{:S(2)}, u32[]{:S(2)}) async-start(s32[64,1,128]{2,1,0:T(1,128)} %broadcast_in_dim.114), calls=%async_computation | async-start | bytes 65536 | tf_op jit(solution)/shard_map/all_to_all | solution.py:24
  163.1 0.3 copy.134
  163.4 0.3 copy.143
  163.7 0.3 copy.145
  164.0 1.5 reduce_sum.83
  165.5 7.3 all-gather.1
  173.1 0.4 fusion.41
  173.5 1.3 convolution_bitcast_fusion.1
  174.8 2.7 copy.142
  177.5 0.2 fusion.29
  177.7 44.0 %all-gather.25.cloned.1.call-done = bf16[8,8,2,40,512]{4,3,2,1,0:T(8,128)(2,1)} async-done(((bf16[2,8,2,40,512]{4,3,2,1,0:T(8,128)(2,1)}), bf16[8,8,2,40,512]{4,3,2,1,0:T(8,128)(2,1)}) %all-gather.25.cloned.1.call-update) | async-done | bytes 5242896 | tf_op jit(solution)/shard_map/all_gather | solution.py:48
  221.7 5.3 copy.139
  227.0 71.0 %all-gather.29.cloned.1.call-done = bf16[16,4,2,40,512]{4,3,2,1,0:T(8,128)(2,1)} async-done(((bf16[8,4,2,40,512]{4,3,2,1,0:T(8,128)(2,1)}), bf16[16,4,2,40,512]{4,3,2,1,0:T(8,128)(2,1)}) %all-gather.29.cloned.1.call-update) | async-done | bytes 5242896 | tf_op jit(solution)/shard_map/all_gather | solution.py:48
  298.0 5.3 copy.140
  303.3 72.0 %all-gather.31.cloned.1.call-done = bf16[32,2,2,48,512]{4,3,2,1,0:T(8,128)(2,1)} async-done(((bf16[4,2,2,48,512]{4,3,2,1,0:T(8,128)(2,1)}), bf16[32,2,2,48,512]{4,3,2,1,0:T(8,128)(2,1)}) %all-gather.31.cloned.1.call-update) | async-done | bytes 6291472 | tf_op jit(solution)/shard_map/all_gather | solution.py:48
  375.2 13.6 %maximum_bitcast_fusion = bf16[2,64,128,512]{3,2,0,1:T(8,128)(2,1)} fusion(bf16[64,2,48,512]{3,2,1,0:T(8,128)(2,1)} %bitcast.143, bf16[64,2,40,512]{3,2,1,0:T(8,128)(2,1)} %bitcast.135, bf16[64,2,40,512]{3,2,1,0:T(8,128)(2,1)} %bitcast.134), kind=kLoop, calls=%fused_computation.24 | loop fusion | flops 50331648 | bytes 33554432 | tf_op jit(solution)/shard_map/transpose | solution.py:17
  388.9 23.2 %copy.141 = bf16[2,64,128,512]{2,1,3,0:T(8,128)(2,1)} copy(bf16[2,64,128,512]{3,2,0,1:T(8,128)(2,1)} %maximum_bitcast_fusion) | data formatting | bytes 33554432 | tf_op jit(solution)/shard_map/transpose | solution.py:17
  412.0 25.3 %reshape.118 = bf16[2,8192,512]{1,2,0:T(8,128)(2,1)} reshape(bf16[2,64,128,512]{2,1,3,0:T(8,128)(2,1)} %copy.141) | data formatting | bytes 33554432 | tf_op jit(solution)/shard_map/reshape | solution.py:19
  437.4 31.6 %while.18 = (s32[]{:T(128)}, f32[128,4,4]{0,2,1:T(4,128)S(1)}, f32[128,4,4]{0,2,1:T(4,128)S(1)}, f32[128,4,4,128]{3,0,2,1:T(8,128)}, s32[8192]{0:T(1024)S(1)}, /...) while((s32[]{:T(128)}, f32[128,4,4]{0,2,1:T(4,128)S(1)}, ...), condition=%wide.region_11.12_spmd.clone, body=%wide.region_5.11_spmd.clone.sunk | while | flops 549196416 | bytes 27144060 | solution.py:154
  437.5 0.8 fusion.53
  439.0 5.6 conditional.3
  439.0 1.3 constant_dynamic-slice_fusion.1
  440.3 0.9 fusion.2
  441.1 0.9 fusion.6
  442.0 1.5 fusion.16
  443.6 1.0 copy-done.1
  444.6 0.8 fusion.53
  446.3 0.8 fusion.53
  447.9 0.8 fusion.53
  449.5 0.8 fusion.53
  451.2 0.8 fusion.53
  452.8 0.8 fusion.53
  454.4 0.8 fusion.53
  456.1 0.8 fusion.53
  457.7 0.8 fusion.53
  459.3 0.8 fusion.53
  461.0 0.8 fusion.53
  462.6 0.8 fusion.53
  464.2 0.8 fusion.53
  465.9 0.8 fusion.53
  467.5 0.8 fusion.53
  469.0 2.5 copy.144
  471.5 1.3 divide_convert_fusion
  472.9 0.2 multiply_reduce_fusion
  473.1 0.3 fusion.31
  473.4 0.5 fusion.27
  474.0 0.1 copy.151
  474.2 1.7 broadcast_select_fusion.1
  476.0 1.0 copy.152
  477.0 332.5 %all-reduce.3.cloned.1.call-done = (f32[4,128,512]{2,1,0:T(8,128)}, f32[4,128,512]{2,1,0:T(8,128)}) async-done(((f32[4,128,512]{2,1,0:T(8,128)}, f32[4,128,512]{2,1,0:T(8,128)}), (f32[4,128,512]{2,1,0:T(8,128)}, f32[4,128,512]{2,1,0:T(8,128)})) %all-reduce.3.cloned.1.call-update) | async-done | bytes 2097168 | tf_op jit(solution)/shard_map/psum | solution.py:188
  809.6 3.0 select_reduce_fusion
  (107 shorter events, 2.8 us)
Async XLA Ops:
  7.2 53.5 %all-gather.19.cloned.1.call-start = ((), (), s32[]{:S(2)}) async-start(), calls=%async_computation.1 | async-start | bytes 2359296 | tf_op jit(solution)/shard_map/all_gather | solution.py:36
  12.8 75.0 %all-gather.23.cloned.1.call-start = ((), (), s32[]{:S(2)}) async-start(), calls=%async_computation.3 | async-start | bytes 1966080 | tf_op jit(solution)/shard_map/all_gather | solution.py:48
  47.5 85.3 %all-gather.27.cloned.1.call-start = ((), (), s32[]{:S(2)}) async-start(), calls=%async_computation.5 | async-start | bytes 2949120 | tf_op jit(solution)/shard_map/all_gather | solution.py:48
  60.6 93.3 %copy-start.4 = (s32[1,128]{1,0:T(1,128)S(1)}, s32[1,128]{1,0:T(1,128)}, u32[]{:S(2)}) copy-start(s32[1,128]{1,0:T(1,128)} %param.15) | copy-start | bytes 1540
  60.6 102.5 %copy-start.2 = (bf16[1,128,2048]{2,1,0:T(8,128)(2,1)S(1)}, bf16[1,128,2048]{2,1,0:T(8,128)(2,1)}, u32[]{:S(2)}) copy-start(bf16[1,128,2048]{2,1,0:T(8,128)(2,1)} %param.12) | copy-start | bytes 1572868
  60.6 103.4 %all-gather.21.cloned.1.call-start = ((), (), s32[]{:S(2)}) async-start(), calls=%async_computation.2 | async-start | bytes 1310720 | tf_op jit(solution)/shard_map/all_gather | solution.py:36
  63.4 158.3 %all-gather.25.cloned.1.call-start = ((), (), s32[]{:S(2)}) async-start(), calls=%async_computation.4 | async-start | bytes 6553600 | tf_op jit(solution)/shard_map/all_gather | solution.py:48
  87.8 75.9 %copy-start.3 = (bf16[1,128,2048]{2,1,0:T(8,128)(2,1)S(1)}, bf16[1,128,2048]{2,1,0:T(8,128)(2,1)}, u32[]{:S(2)}) copy-start(bf16[1,128,2048]{2,1,0:T(8,128)(2,1)} %param.19) | copy-start | bytes 1572868
  87.8 210.1 %all-gather.29.cloned.1.call-start = ((), (), s32[]{:S(2)}) async-start(), calls=%async_computation.6 | async-start | bytes 7864320 | tf_op jit(solution)/shard_map/all_gather | solution.py:48
  132.8 242.4 %all-gather.31.cloned.1.call-start = ((), (), s32[]{:S(2)}) async-start(), calls=%async_computation.7 | async-start | bytes 7077888 | tf_op jit(solution)/shard_map/all_gather | solution.py:48
  154.5 282.8 %all-to-all-start = ((s32[64,1,128]{2,1,0:T(1,128)}), s32[64,1,128]{2,1,0:T(1,128)S(1)}, u32[]{:S(2)}, u32[]{:S(2)}) async-start(s32[64,1,128]{2,1,0:T(1,128)} %broadcast_in_dim.114), calls=%async_computation | async-start | bytes 65536 | tf_op jit(solution)/shard_map/all_to_all | solution.py:24
  163.0 646.5 %all-reduce.3.cloned.1.call-start = ((), (), s32[]{:S(2)}) async-start(), calls=%async_computation.8 | async-start | bytes 4194304 | tf_op jit(solution)/shard_map/psum | solution.py:188
  440.3 1.8 copy-start
  443.6 1.0 copy-start.1
  473.4 2.5 copy-start.5
Sparse Core Ops, SparseCore 0:
  13.0 45.0 all-gather.18
  59.8 27.9 all-gather.22
  89.6 43.1 all-gather.26
  135.0 24.7 all-gather.20
  161.5 60.1 all-gather.24
  223.3 74.6 all-gather.28
  299.8 75.3 all-gather.30
  476.1 333.4 all-reduce.2
